TPU v7x, 256 devices: a whole 4x4x8 slice. The times are simulated.
256 devices in a mesh: dp: 4 (over y), expert: 8 (over z), mp: 8 (over x, core).
Axes of the slice: x: 4, y: 4, z: 8, core: 2. Of those that a mesh axis runs over, the one named last changes fastest.
Arguments:
- base_weights: bfloat16 [16, 2560, 3072], P('expert', None, 'mp'), may hold values from -6 to 6
- delta_blocks: bfloat16 [32768, 128, 128], P(('dp', 'expert', 'mp')), may hold values from -4 to 4
- block_ids: int32 [32768], P(('dp', 'expert', 'mp')), may hold values from 0 to 7679, as said below
- block_counts: int32 [16384], P(('dp', 'expert', 'mp')), may hold values from 0 to 2, as said below
- owner_map: int32 [16], replicated, may hold values from 0 to 15, as said below
Outputs:
- merged_weights: bfloat16 [16, 2560, 3072], P('expert', None, 'mp')
Inputs may be any that keep to these rules, and one draw needn't show every extreme that they name: A permutation: expert e is held in serving position owner_map[e], by the serving group owner_map[e] // 2. `block_ids`: every slot of device s for owner q, used or not, names a block (e * 20 + r) * 24 + c with owner_map[e] // 2 == q // 8 and c // 3 == q % 8. Names may repeat within and across devices. `block_counts`: at most 2 used slots from one device to one owner; in every draw some owner receives exactly 2 blocks from every device.
All inputs are finite; a program needn't handle non-finite values.
Results may differ from a plain program's by a relative error of at most 0.001.
Values may be sent and summed in bfloat16 or wider, within the bound.
A program may use at most 128 MiB of HBM per device.

v0:
```python
import jax
import jax.numpy as jnp
from jax import lax
from jax.sharding import PartitionSpec as P


def to_matrix(summed, exp_dev, row_blocks, col_blocks, block_size):
    grid = summed.reshape(exp_dev, row_blocks, col_blocks, block_size, block_size)
    return grid.transpose(0, 1, 3, 2, 4).reshape(
        exp_dev, row_blocks * block_size, col_blocks * block_size
    )


def body(base_weights, delta_blocks, block_ids, block_counts, owner_map):
    exp_dev, row_count, col_count = base_weights.shape
    block_size = delta_blocks.shape[1]
    row_blocks = row_count // block_size
    col_blocks = col_count // block_size
    col_total = col_blocks * lax.axis_size("mp")
    slot_total = delta_blocks.shape[0]
    capacity = slot_total // block_counts.shape[0]
    active = jnp.arange(slot_total, dtype=jnp.int32) % capacity < jnp.repeat(block_counts, capacity)
    values = jnp.where(active[:, None, None], delta_blocks, jnp.zeros((), jnp.bfloat16))
    expert = block_ids // (row_blocks * col_total)
    remain = block_ids % (row_blocks * col_total)
    row_index = remain // col_total
    col_index = remain % col_total
    expert_count = owner_map.shape[0]
    matches = expert[:, None] == jnp.arange(expert_count, dtype=jnp.int32)[None, :]
    position = jnp.sum(jnp.where(matches, owner_map[None, :], 0), axis=1)
    idents = (position % exp_dev * row_blocks + row_index) * col_blocks + col_index % col_blocks
    arrived = lax.all_to_all(values, ("expert", "mp"), split_axis=0, concat_axis=0, tiled=True)
    arrived_ids = lax.all_to_all(idents, ("expert", "mp"), split_axis=0, concat_axis=0, tiled=True)
    empty = jnp.zeros((exp_dev * row_blocks * col_blocks, block_size, block_size), jnp.float32)
    own_sum = empty.at[arrived_ids].add(arrived.astype(jnp.float32))
    own_delta = to_matrix(own_sum, exp_dev, row_blocks, col_blocks, block_size)
    quarter = lax.psum_scatter(own_delta, "dp", scatter_dimension=1, tiled=True)
    row_share = quarter.shape[1]
    base_part = lax.dynamic_slice_in_dim(
        base_weights, lax.axis_index("dp") * row_share, row_share, 1
    )
    merged_part = (base_part.astype(jnp.float32) + quarter).astype(jnp.bfloat16)
    return lax.all_gather(merged_part, "dp", axis=1, tiled=True)


def solution(mesh):
    in_specs = (
        P("expert", None, "mp"),
        P(("dp", "expert", "mp"), None, None),
        P(("dp", "expert", "mp")),
        P(("dp", "expert", "mp")),
        P(),
    )
    out_specs = P("expert", None, "mp")
    return jax.shard_map(body, mesh=mesh, in_specs=in_specs, out_specs=out_specs, check_vma=False)
```

profile of v0, /device:TPU:32, one launch (start us, length us, event | category | flops | bytes accessed | tf_op | source)
XLA Modules:
  0.0 328.9 jit_solution(5700634134703606456)
XLA Ops:
  6.5 0.7 and_select_fusion.6
  7.2 0.7 select_reduce_fusion
  7.9 0.7 fusion
  8.6 0.8 all_to_all.11
  9.4 11.6 %all-to-all-start = ((s32[64,2,1]{1,2,0:T(1,128)}), s32[64,2,1]{1,2,0:T(1,128)S(1)}, u32[]{:S(2)}, u32[]{:S(2)}) async-start(s32[64,2,1]{1,2,0:T(1,128)} %bitcast), calls=%async_computation | async-start | bytes 65536 | tf_op jit(solution)/shard_map/all_to_all | solution.py:33
  21.0 0.7 broadcast_in_dim.38
  21.7 0.1 reshape.55
  21.9 4.5 %broadcast_select_fusion = bf16[128,128,128]{2,1,0:T(8,128)(2,1)} fusion(bf16[128,128,128]{2,1,0:T(8,128)(2,1)} %param.6, pred[128]{0:T(512)(128)(4,1)S(1)} %fusion.1), kind=kLoop, calls=%fused_computation.1 | loop fusion | flops 2097152 | bytes 8388736 | tf_op jit(solution)/shard_map/jit(_where)/select_n | solution.py:23
  26.3 3.2 all-to-all-done
  29.6 7.3 %all-to-all-start.1 = ((bf16[128,128,128]{2,1,0:T(8,128)(2,1)}), bf16[128,128,128]{2,1,0:T(8,128)(2,1)}, u32[]{:S(2)}, u32[]{:S(2)}) async-start(bf16[128,128,128]{2,1,0:T(8,128)(2,1)} %broadcast_select_fusion), calls=%async_computation.1 | async-start | bytes 8388608 | tf_op jit(solution)/shard_map/all_to_all | solution.py:32
  36.8 0.0 reduce-scatter.2.cloned.1.call-start
  36.9 0.5 broadcast.48
  37.4 0.7 reduce.3
  38.1 0.1 all_to_all.13
  38.3 93.8 %all-to-all-done.1 = bf16[128,128,128]{2,1,0:T(8,128)(2,1)} async-done(((bf16[128,128,128]{2,1,0:T(8,128)(2,1)}), bf16[128,128,128]{2,1,0:T(8,128)(2,1)}, u32[]{:S(2)}, u32[]{:S(2)}) %all-to-all-start.1) | async-done | bytes 4194336 | tf_op jit(solution)/shard_map/all_to_all | solution.py:32
  132.1 6.5 %convert_element_type.10 = f32[128,128,128]{2,1,0:T(8,128)} convert(bf16[128,128,128]{2,1,0:T(8,128)(2,1)} %all-to-all-done.1) | non-fusion elementwise | flops 2097152 | bytes 12582912 | tf_op jit(solution)/shard_map/convert_element_type | solution.py:35
  138.6 4.1 %broadcast_in_dim.35 = f32[120,128,128]{2,1,0:T(8,128)} broadcast(f32[]{:T(128)} %constant.67.clone.1), dimensions={} | broadcast | bytes 7864324 | tf_op jit(solution)/shard_map/broadcast_in_dim | solution.py:34
  142.6 26.5 %scatter_fusion = f32[120,128,128]{2,1,0:T(8,128)} fusion(f32[120,128,128]{2,1,0:T(8,128)} %broadcast_in_dim.35, s32[128]{0:T(128)S(1)} %fusion.6, f32[128,128,128]{2,1,0:T(8,128)} %convert_element_type.10), kind=kCustom, calls=%fused_computation | custom fusion | flops 2097152 | bytes 25166336 | tf_op jit(solution)/shard_map/scatter-add | solution.py:35
  169.1 9.2 %copy.15 = f32[2,20,128,3,128]{2,1,4,3,0:T(8,128)} copy(f32[2,20,128,3,128]{4,2,3,1,0:T(8,128)} %bitcast.9) | data formatting | bytes 15728640 | tf_op jit(solution)/shard_map/transpose | solution.py:9
  178.2 9.3 %reshape.57 = f32[2,2560,384]{1,2,0:T(8,128)} reshape(f32[2,20,128,3,128]{2,1,4,3,0:T(8,128)} %copy.15) | data formatting | bytes 15728640 | tf_op jit(solution)/shard_map/reshape | solution.py:9
  187.5 0.0 reduce-scatter.2.cloned.1.call-update
  187.6 0.0 all-gather.2.cloned.1.call-start
  187.6 1.3 constant_dynamic-slice_fusion
  188.9 0.6 copy.17
  189.6 75.0 %reduce-scatter.2.cloned.1.call-done = f32[2,640,384]{1,2,0:T(8,128)} async-done(((f32[2,2560,384]{1,2,0:T(8,128)}), f32[2,640,384]{1,2,0:T(8,128)}) %reduce-scatter.2.cloned.1.call-update) | async-done | bytes 1966096 | tf_op jit(solution)/shard_map/reduce_scatter | solution.py:37
  264.5 2.7 add_convert_fusion
  267.2 0.0 all-gather.2.cloned.1.call-update
  267.2 48.5 %all-gather.2.cloned.1.call-done = bf16[2,2560,384]{1,2,0:T(8,128)(2,1)} async-done(((bf16[2,640,384]{1,2,0:T(8,128)(2,1)}), bf16[2,2560,384]{1,2,0:T(8,128)(2,1)}) %all-gather.2.cloned.1.call-update) | async-done | bytes 3932176 | tf_op jit(solution)/shard_map/all_gather | solution.py:43
  315.7 6.3 %copy.16 = bf16[2,2560,384]{2,1,0:T(8,128)(2,1)} copy(bf16[2,2560,384]{1,2,0:T(8,128)(2,1)} %all-gather.2.cloned.1.call-done) | data formatting | bytes 7864320 | tf_op jit(solution)/shard_map/all_gather | solution.py:43
  (2 shorter events, 0.0 us)
Async XLA Ops:
  9.4 20.2 %all-to-all-start = ((s32[64,2,1]{1,2,0:T(1,128)}), s32[64,2,1]{1,2,0:T(1,128)S(1)}, u32[]{:S(2)}, u32[]{:S(2)}) async-start(s32[64,2,1]{1,2,0:T(1,128)} %bitcast), calls=%async_computation | async-start | bytes 65536 | tf_op jit(solution)/shard_map/all_to_all | solution.py:33
  29.6 102.5 %all-to-all-start.1 = ((bf16[128,128,128]{2,1,0:T(8,128)(2,1)}), bf16[128,128,128]{2,1,0:T(8,128)(2,1)}, u32[]{:S(2)}, u32[]{:S(2)}) async-start(bf16[128,128,128]{2,1,0:T(8,128)(2,1)} %broadcast_select_fusion), calls=%async_computation.1 | async-start | bytes 8388608 | tf_op jit(solution)/shard_map/all_to_all | solution.py:32
  36.8 227.7 %reduce-scatter.2.cloned.1.call-start = ((), (), s32[]{:S(2)}) async-start(), calls=%async_computation.3 | async-start | bytes 9830400 | tf_op jit(solution)/shard_map/reduce_scatter | solution.py:37
  187.6 128.2 %all-gather.2.cloned.1.call-start = ((), (), s32[]{:S(2)}) async-start(), calls=%async_computation.4 | async-start | bytes 4915200 | tf_op jit(solution)/shard_map/all_gather | solution.py:43
Sparse Core Ops, SparseCore 0:
  187.7 76.8 reduce-scatter.1
  267.4 48.3 all-gather.1
where the time goes:
time: 331 us; the launch traced here: 329 us
  waiting for transfers between devices  221 us (67%)
  other arithmetic  42.9 us (13%)
  local copies, waits for them, and re-layouts  33 us (10%)
  starting transfers between devices  18.9 us (6%)
  between operations  13.5 us (4%)
    all_to_all x1, waiting for transfers between devices, body(): lax.all_to_all(values, ('expert', 'mp'), split_axis=0, concat_axis=0, til...  93.8 us
    reduce_scatter x1, waiting for transfers between devices, body(): quarter = lax.psum_scatter(own_delta, 'dp', scatter_dimension=1, tiled=True)  75 us
    all_gather x1, waiting for transfers between devices, body(): return lax.all_gather(merged_part, 'dp', axis=1, tiled=True)  48.5 us
    scatter-add x1, other arithmetic, body(): own_sum = empty.at[arrived_ids].add(arrived.astype(jnp.float32))  26.5 us
    all_to_all x1, starting transfers between devices, body(): lax.all_to_all(idents, ('expert', 'mp'), split_axis=0, concat_axis=0, til...  11.6 us
    reshape x1, local copies, waits for them, and re-layouts, to_matrix(): grid.transpose(0, 1, 3, 2, 4)  9.28 us
    transpose x1, local copies, waits for them, and re-layouts, to_matrix(): grid.transpose(0, 1, 3, 2, 4)  9.15 us
    all_to_all x1, starting transfers between devices, body(): lax.all_to_all(values, ('expert', 'mp'), split_axis=0, concat_axis=0, til...  7.27 us
  transfers between devices with their start and end apart: 4, of which 4 were waited for; matrix products, arithmetic and copies ran while one was open for 3% of the time, Pallas kernels for 0%

commit v1 on v0

v1 whole, which is shorter than its diff:
```python
import functools

import jax
import jax.numpy as jnp
from jax import lax
from jax.experimental import pallas as pl
from jax.experimental.pallas import tpu as pltpu
from jax.sharding import PartitionSpec as P

MESH = pl.DeviceIdType.MESH
ROWS = 8
LANES = 128


def kernel(
    cfg,
    owner_map_ref,
    base_hbm,
    delta_hbm,
    ids_ref,
    counts_ref,
    out_hbm,
    *scratch,
):
    n_dp, n_ex, n_mp, exp_dev, row_blocks, col_blocks, capacity, chunks = cfg
    recv = scratch[:chunks]
    (
    base_vmem,
    partial,
    stage,
    enc,
    keys,
    keys_t,
    table,
    order,
    a2a_send,
    a2a_recv,
    ids_send,
    ids_recv,
    local_sem,
    gather_send,
    gather_recv,
    ) = scratch[chunks:]
    n_dev = n_dp * n_ex * n_mp
    n_slots = n_dev * capacity
    quarter = chunks * ROWS
    positions = exp_dev * row_blocks * col_blocks
    col_total = col_blocks * n_mp
    d = lax.axis_index("dp")
    e = lax.axis_index("expert")
    m = lax.axis_index("mp")
    me = (d * n_ex + e) * n_mp + m

    barrier = pltpu.get_barrier_semaphore()
    ds = [lax.rem(d + i, n_dp) for i in range(n_dp)]
    es = [lax.rem(e + i, n_ex) for i in range(n_ex)]

    def greet(i, carry):
        m2 = lax.rem(m + i, n_mp)
        for j in range(n_dp):
            for k in range(n_ex):
                pl.semaphore_signal(barrier, inc=1, device_id=(ds[j], es[k], m2), device_id_type=MESH)
        return carry

    for j in range(n_dp):
        for k in range(n_ex):
            if j or k:
                pl.semaphore_signal(barrier, inc=1, device_id=(ds[j], es[k], m), device_id_type=MESH)
    lax.fori_loop(1, n_mp, greet, 0)

    base_copy = pltpu.make_async_copy(base_hbm.at[:, :, pl.ds(d * quarter, quarter), :], base_vmem, local_sem.at[0])
    base_copy.start()

    ids = ids_ref[...].astype(jnp.float32)
    per_expert = row_blocks * col_total
    expert = jnp.floor((ids + 0.5) * (1.0 / per_expert))
    remain = ids - expert * per_expert
    row_index = jnp.floor((remain + 0.5) * (1.0 / col_total))
    col_index = remain - row_index * col_total
    part = jnp.floor((col_index + 0.5) * (1.0 / col_blocks))
    local_col = col_index - part * col_blocks
    local_expert = jnp.zeros_like(ids)
    for i in range(n_ex * exp_dev):
        local_expert = jnp.where(expert == i, lax.rem(owner_map_ref[i], exp_dev).astype(jnp.float32), local_expert)
    place = (local_expert * row_blocks + row_index) * col_blocks + local_col
    owners = counts_ref.shape[1]
    spread = (
        lax.broadcasted_iota(jnp.int32, (owners, LANES), 1) // capacity
        == lax.broadcasted_iota(jnp.int32, (owners, LANES), 0)
    ).astype(jnp.float32)
    used = jnp.dot(
        jnp.broadcast_to(counts_ref[...].astype(jnp.float32), (8, owners)), spread, preferred_element_type=jnp.float32
    )[0:1, :]
    slot_k = lax.broadcasted_iota(jnp.int32, (1, LANES), 1) % capacity
    place = jnp.where(slot_k.astype(jnp.float32) < used, place, float(positions))
    enc[...] = place.astype(jnp.int32)

    pl.semaphore_wait(barrier, n_dev - 1)

    z_order = []
    for i in range(1, n_ex // 2):
        z_order += [i, n_ex - i]
    z_order.append(n_ex // 2)

    def send_block(c, d2, e2, m2, with_ids):
        q = e2 * n_mp + m2
        pltpu.make_async_remote_copy(
            src_ref=delta_hbm.at[pl.ds(q * capacity, capacity), pl.ds(d2 * quarter + c * ROWS, ROWS), :],
            dst_ref=recv[c].at[pl.ds(me * capacity, capacity)],
            send_sem=a2a_send.at[c],
            recv_sem=a2a_recv.at[c],
            device_id=(d2, e2, m2),
            device_id_type=MESH,
        ).start()
        if with_ids:
            pltpu.make_async_remote_copy(
                src_ref=enc,
                dst_ref=keys.at[me],
                send_sem=ids_send,
                recv_sem=ids_recv,
                device_id=(d2, e2, m2),
                device_id_type=MESH,
            ).start()

    def exchange(c):
        with_ids = c == 0
        for k in z_order:
            send_block(c, d, es[k], m, with_ids)
        mine = e * n_mp + m
        pltpu.make_async_copy(
            delta_hbm.at[pl.ds(mine * capacity, capacity), pl.ds(d * quarter + c * ROWS, ROWS), :],
            recv[c].at[pl.ds(me * capacity, capacity)],
            a2a_recv.at[c],
        ).start()

        def step(r, carry):
            d2 = lax.rem(d + r // n_mp, n_dp)
            m2 = lax.rem(m + r, n_mp)
            for k in z_order + [0]:
                send_block(c, d2, es[k], m2, with_ids)
            return carry

        lax.fori_loop(1, n_dp * n_mp, step, 0)

    exchange(0)
    keys[pl.ds(me, 1)] = enc[...].reshape(1, 1, LANES)
    if chunks > 1:
        exchange(1)
    base_copy.wait()

    others = keys.at[pl.ds(0, n_dev - 1)]
    pltpu.make_async_copy(others, others, ids_recv).wait()
    all_keys = keys[...].reshape(n_dev, LANES)
    q_mine = e * n_mp + m
    for g in range(n_dev // LANES):
        keys_t[:, g * LANES : (g + 1) * LANES] = all_keys[g * LANES : (g + 1) * LANES, :].T
    lane = lax.broadcasted_iota(jnp.int32, (1, LANES), 1)
    row_keys, row_slots = [], []
    for k in range(capacity):
        row = keys_t[pl.ds(q_mine * capacity + k, 1), :]
        for g in range(n_dev // LANES):
            row_keys.append(row[:, g * LANES : (g + 1) * LANES])
            row_slots.append((g * LANES + lane) * capacity + k)
    groups = len(row_keys)

    def down(row):
        return jnp.broadcast_to(row, (LANES, LANES)).T

    row_mixed = [a * n_slots + b for a, b in zip(row_keys, row_slots)]
    col_keys = [down(a) for a in row_keys]
    col_slots = [down(a) for a in row_slots]
    col_mixed = [a * n_slots + b for a, b in zip(col_keys, col_slots)]

    def count(masks):
        total = sum(jnp.where(x, 1, 0) for x in masks)
        return jnp.sum(total, axis=0, keepdims=True)

    ranks = [count([col_mixed[h] < row_mixed[g] for h in range(groups)]) for g in range(groups)]
    col_ranks = [down(a) for a in ranks]
    for g in range(groups):
        want = g * LANES + lane
        hit = [col_ranks[h] == want for h in range(groups)]
        table[g : g + 1, :] = jnp.sum(sum(jnp.where(x, s, 0) for x, s in zip(hit, col_slots)), axis=0, keepdims=True)
        table[groups + g : groups + g + 1, :] = jnp.sum(
            sum(jnp.where(x, s, 0) for x, s in zip(hit, col_keys)), axis=0, keepdims=True
        )
    table[2 * groups : 2 * groups + 1, :] = jnp.maximum(count([x <= lane for x in col_keys]) - 1, 0)
    table[2 * groups + 1 : 2 * groups + 2, :] = count([x == lane for x in col_keys])

    peers = [lax.rem(d + i, n_dp) for i in range(1, n_dp)]

    for c in range(chunks):
        if c == 0:
            to_smem = pltpu.make_async_copy(table, order, local_sem.at[1])
            to_smem.start()
            to_smem.wait()
        pltpu.make_async_copy(recv[c], recv[c], a2a_recv.at[c]).wait()

        def add(j, carry):
            running, before = carry
            g = j // LANES
            l = j % LANES
            slot = order[g, l]
            key = order[groups + g, l]
            block = recv[c][slot].astype(jnp.float32)
            running = jnp.where(key == before, running, 0.0) + block
            partial[j] = running
            return running, key

        lax.fori_loop(0, n_slots, add, (jnp.zeros((ROWS, LANES), jnp.float32), jnp.int32(-1)), unroll=8)

        def finish(i, carry):
            a = i // row_blocks
            b = i % row_blocks
            for k in range(col_blocks):
                p = i * col_blocks + k
                total = partial[order[2 * groups, p]]
                total = jnp.where(order[2 * groups + 1, p] > 0, total, 0.0)
                old = base_vmem[a, b, c * ROWS : (c + 1) * ROWS, k * LANES : (k + 1) * LANES]
                stage[c, a, b, :, k * LANES : (k + 1) * LANES] = (old.astype(jnp.float32) + total).astype(jnp.bfloat16)
            return carry

        lax.fori_loop(0, exp_dev * row_blocks, finish, 0, unroll=4)
        if c + 2 < chunks:
            exchange(c + 2)
        place_rows = pl.ds(d * quarter + c * ROWS, ROWS)
        for d2 in peers:
            pltpu.make_async_remote_copy(
                src_ref=stage.at[c],
                dst_ref=out_hbm.at[:, :, place_rows, :],
                send_sem=gather_send,
                recv_sem=gather_recv,
                device_id=(d2, e, m),
                device_id_type=MESH,
            ).start()
        pltpu.make_async_copy(stage.at[c], out_hbm.at[:, :, place_rows, :], gather_recv).start()

    pltpu.make_async_copy(out_hbm, out_hbm, gather_recv).wait()
    sent = out_hbm.at[:, :, pl.ds(0, (n_dp - 1) * quarter), :]
    pltpu.make_async_copy(sent, sent, gather_send).wait()
    for c in range(chunks):
        sent = recv[c].at[pl.ds(0, n_slots - capacity)]
        pltpu.make_async_copy(sent, sent, a2a_send.at[c]).wait()
    pltpu.make_async_copy(others, others, ids_send).wait()


def body(base_weights, delta_blocks, block_ids, block_counts, owner_map):
    n_dp, n_ex, n_mp = (lax.axis_size(a) for a in ("dp", "expert", "mp"))
    n_dev = n_dp * n_ex * n_mp
    exp_dev, row_count, col_count = base_weights.shape
    block_size = delta_blocks.shape[1]
    row_blocks = row_count // block_size
    col_blocks = col_count // block_size
    capacity = delta_blocks.shape[0] // block_counts.shape[0]
    quarter = block_size // n_dp
    chunks = quarter // ROWS
    n_slots = n_dev * capacity
    cfg = (n_dp, n_ex, n_mp, exp_dev, row_blocks, col_blocks, capacity, chunks)
    shape = (exp_dev, row_blocks, block_size, col_count)
    merged = pl.pallas_call(
        functools.partial(kernel, cfg),
        out_shape=jax.ShapeDtypeStruct(shape, jnp.bfloat16),
        in_specs=[
            pl.BlockSpec(memory_space=pltpu.SMEM),
            pl.BlockSpec(memory_space=pl.ANY),
            pl.BlockSpec(memory_space=pl.ANY),
            pl.BlockSpec(memory_space=pltpu.VMEM),
            pl.BlockSpec(memory_space=pltpu.VMEM),
        ],
        out_specs=pl.BlockSpec(memory_space=pl.ANY),
        scratch_shapes=[
            *[pltpu.VMEM((n_slots, ROWS, LANES), jnp.bfloat16)] * chunks,
            pltpu.VMEM((exp_dev, row_blocks, quarter, col_count), jnp.bfloat16),
            pltpu.VMEM((n_slots, ROWS, LANES), jnp.float32),
            pltpu.VMEM((chunks, exp_dev, row_blocks, ROWS, col_count), jnp.bfloat16),
            pltpu.VMEM((1, LANES), jnp.int32),
            pltpu.VMEM((n_dev, 1, LANES), jnp.int32),
            pltpu.VMEM((LANES, n_dev), jnp.int32),
            pltpu.VMEM((16, LANES), jnp.int32),
            pltpu.SMEM((16, LANES), jnp.int32),
            pltpu.SemaphoreType.DMA((chunks,)),
            pltpu.SemaphoreType.DMA((chunks,)),
            pltpu.SemaphoreType.DMA,
            pltpu.SemaphoreType.DMA,
            pltpu.SemaphoreType.DMA((2,)),
            pltpu.SemaphoreType.DMA,
            pltpu.SemaphoreType.DMA,
        ],
        compiler_params=pltpu.CompilerParams(
            collective_id=0, has_side_effects=True, vmem_limit_bytes=48 * 2**20
        ),
        name="merge_blocks",
    )(
        owner_map,
        base_weights.reshape(shape),
        delta_blocks,
        block_ids.reshape(1, -1),
        block_counts.reshape(1, -1),
    )
    return merged.reshape(base_weights.shape)


def solution(mesh):
    in_specs = (
        P("expert", None, "mp"),
        P(("dp", "expert", "mp"), None, None),
        P(("dp", "expert", "mp")),
        P(("dp", "expert", "mp")),
        P(),
    )
    out_specs = P("expert", None, "mp")
    return jax.shard_map(body, mesh=mesh, in_specs=in_specs, out_specs=out_specs, check_vma=False)
```

time: 331 us -> 135 us (0.41)
  waiting for transfers between devices: 221 us -> 0 us
  Pallas kernels: 0 us -> 130 us
  other arithmetic: 42.9 us -> 0 us
  local copies, waits for them, and re-layouts: 33 us -> 3.89 us
  starting transfers between devices: 18.9 us -> 0 us
  between operations: 13.5 us -> 0.01 us
    pallas_call x0 -> x1, Pallas kernels: none -> 130 us  [body(): pl.pallas_call(functools.partial(kernel, cfg), out_shape=jax.ShapeDtypeSt...]
    all_to_all x2 -> x0, waiting for transfers between devices: 97 us -> none  [the longest x1 93.8 us: body(): lax.all_to_all(values, ('expert', 'mp'), split_axis=0, concat_axis=0, til...]
    reduce_scatter x1 -> x0, waiting for transfers between devices: 75 us -> none  [body(): quarter = lax.psum_scatter(own_delta, 'dp', scatter_dimension=1, tiled=True)]
    all_gather x1 -> x0, waiting for transfers between devices: 48.5 us -> none  [body(): return lax.all_gather(merged_part, 'dp', axis=1, tiled=True)]
    scatter-add x1 -> x0, other arithmetic: 26.5 us -> none  [body(): own_sum = empty.at[arrived_ids].add(arrived.astype(jnp.float32))]
    all_to_all x2 -> x0, starting transfers between devices: 18.9 us -> none  [the longest x1 11.6 us: body(): lax.all_to_all(idents, ('expert', 'mp'), split_axis=0, concat_axis=0, til...]
    reshape x2 -> x0, local copies, waits for them, and re-layouts: 9.42 us -> none  [the longest x1 9.28 us: to_matrix(): grid.transpose(0, 1, 3, 2, 4)]
    transpose x1 -> x0, local copies, waits for them, and re-layouts: 9.15 us -> none  [to_matrix(): grid.transpose(0, 1, 3, 2, 4)]
  transfers between devices with their start and end apart: 4 -> 0, of which waited for: 4 -> 0; matrix products, arithmetic and copies ran while one was open for 3% -> 0% of each run, Pallas kernels for 0% -> 0%
where the time goes in v1:
time: 135 us; the launch traced here: 134 us
  Pallas kernels  130 us (96%)
  local copies, waits for them, and re-layouts  3.89 us (3%)
    pallas_call x1, Pallas kernels, body(): pl.pallas_call(functools.partial(kernel, cfg), out_shape=jax.ShapeDtypeSt...  130 us
    unnamed x7, local copies, waits for them, and re-layouts  3.89 us

profile of v1, /device:TPU:32, one launch (start us, length us, event | category | flops | bytes accessed | tf_op | source)
XLA Modules:
  0.0 134.0 jit_solution(1582107540253444992)
XLA Ops:
  0.0 0.0 copy-start
  0.0 0.7 copy-done
  0.7 0.0 copy-start.1
  0.7 0.7 copy-done.1
  1.3 0.0 copy-start.2
  1.3 0.7 copy-done.2
  2.0 130.1 %merge_blocks.1 = bf16[2,20,128,384]{3,2,1,0:T(8,128)(2,1)S(1)} custom-call(s32[16]{0:T(128)S(1)} %copy-done, bf16[2,20,128,384]{3,2,1,0:T(8,128)(2,1)} %bitcast.7, bf16[128,128,128]{2,1,0:T(8,128)(2,1)} %delta_hbm.1, s32[1,128]{1,0:T(1,128)S(1)} %bitcast.5, s32[1,64]{1,0:T(1,128)S(1)} %bitcast.6), custom_call_target="tpu_custom_call" | custom-call | tf_op jit(solution)/shard_map/merge_blocks/pallas_call | solution.py:260
  132.1 1.9 %copy.7 = bf16[2,2560,384]{2,1,0:T(8,128)(2,1)} copy(bf16[2,2560,384]{2,1,0:T(8,128)(2,1)S(1)} %bitcast.4) | data formatting | bytes 7864320
Async XLA Ops:
  0.0 0.7 copy-start
  0.7 0.7 copy-start.1
  1.3 0.7 copy-start.2

commit v2 on v1

v2 whole, which is shorter than its diff:
```python
import functools

import jax
import jax.numpy as jnp
from jax import lax
from jax.experimental import pallas as pl
from jax.experimental.pallas import tpu as pltpu
from jax.sharding import PartitionSpec as P

MESH = pl.DeviceIdType.MESH
CHUNKS = (8, 8, 8, 8)
AHEAD = 12
GATHER_SPLITS = 10
PER_STEP = 4
UNROLL = 4
LANES = 128


def kernel(
    cfg,
    lists,
    base_hbm,
    delta_hbm,
    out_hbm,
    *scratch,
):
    n_dp, n_ex, n_mp, exp_dev, row_blocks, col_blocks, capacity, chunk_rows = cfg
    chunks = len(chunk_rows)
    first_row = [sum(chunk_rows[:c]) for c in range(chunks)]
    recv = scratch[:chunks]
    stage = scratch[chunks : 2 * chunks]
    (
        base_vmem,
        partial,
        enc,
        column_keys,
        keys,
        keys_t,
        table,
        flags,
        order,
        weight,
        a2a_send,
        a2a_recv,
        ids_send,
        ids_recv,
        local_sem,
        gather_send,
        gather_recv,
        column_sem,
    ) = scratch[2 * chunks :]
    n_dev = n_dp * n_ex * n_mp
    n_slots = n_dev * capacity
    quarter = sum(chunk_rows)
    positions = exp_dev * row_blocks * col_blocks
    col_total = col_blocks * n_mp
    d = lax.axis_index("dp")
    e = lax.axis_index("expert")
    m = lax.axis_index("mp")
    me = (d * n_mp + m) * n_ex + e

    barrier = pltpu.get_barrier_semaphore()
    ds = [lax.rem(d + i, n_dp) for i in range(n_dp)]
    es = [lax.rem(e + i, n_ex) for i in range(n_ex)]
    ms = [lax.rem(m + i, n_mp) for i in range(n_mp)]
    plane = [(ds[i], e, ms[j]) for j in range(n_mp) for i in range(n_dp) if i or j]
    column = [(d, es[k], m) for k in range(1, n_ex)]
    for device in column + plane:
        pl.semaphore_signal(barrier, inc=1, device_id=device, device_id_type=MESH)

    base_copy = pltpu.make_async_copy(base_hbm.at[:, :, pl.ds(d * quarter, quarter), :], base_vmem, local_sem.at[0])
    base_copy.start()

    ids = lists[0:1, :].astype(jnp.float32)
    counts = lists[1:2, :].astype(jnp.float32)
    owners = n_ex * n_mp
    per_expert = row_blocks * col_total
    expert = jnp.floor((ids + 0.5) * (1.0 / per_expert))
    remain = ids - expert * per_expert
    row_index = jnp.floor((remain + 0.5) * (1.0 / col_total))
    col_index = remain - row_index * col_total
    part = jnp.floor((col_index + 0.5) * (1.0 / col_blocks))
    local_col = col_index - part * col_blocks
    local_expert = jnp.zeros_like(ids)
    for i in range(n_ex * exp_dev):
        position = jnp.broadcast_to(counts[:, owners + i : owners + i + 1], (1, LANES))
        inside = position - exp_dev * jnp.floor(position * (1.0 / exp_dev))
        local_expert = jnp.where(expert == float(i), inside, local_expert)
    place = (local_expert * row_blocks + row_index) * col_blocks + local_col
    spread = (
        lax.broadcasted_iota(jnp.int32, (owners, LANES), 1) // capacity
        == lax.broadcasted_iota(jnp.int32, (owners, LANES), 0)
    ).astype(jnp.float32)
    used = jnp.dot(
        jnp.broadcast_to(counts[:, :owners], (8, owners)), spread, preferred_element_type=jnp.float32
    )[0:1, :]
    slot_k = lax.broadcasted_iota(jnp.int32, (1, LANES), 1) % capacity
    place = jnp.where(slot_k.astype(jnp.float32) < used, place, float(positions))
    enc[...] = place.astype(jnp.int32)

    pl.semaphore_wait(barrier, len(column) + len(plane))
    for device in plane:
        pl.semaphore_signal(column_sem, inc=1, device_id=device, device_id_type=MESH)

    z_order = []
    for i in range(1, n_ex // 2):
        z_order += [i, n_ex - i]
    z_order.append(n_ex // 2)

    def send_block(c, d2, e2, m2):
        q = e2 * n_mp + m2
        pltpu.make_async_remote_copy(
            src_ref=delta_hbm.at[pl.ds(q * capacity, capacity), pl.ds(d2 * quarter + first_row[c], chunk_rows[c]), :],
            dst_ref=recv[c].at[pl.ds(me * capacity, capacity)],
            send_sem=a2a_send.at[c],
            recv_sem=a2a_recv.at[c],
            device_id=(d2, e2, m2),
            device_id_type=MESH,
        ).start()
    mine = e * n_mp + m
    x_count = n_mp // 2
    x = m // 2
    core = m % 2

    n_steps = n_dp * n_mp
    last = chunks - 1
    peers = n_dp - 1
    splits = GATHER_SPLITS
    span = row_blocks // splits
    n_pieces = peers * exp_dev * splits
    half = n_steps // 2
    early = half + AHEAD
    rest_steps = n_steps - early

    def own_pair(c):
        pltpu.make_async_copy(
            delta_hbm.at[pl.ds(mine * capacity, capacity), pl.ds(d * quarter + first_row[c], chunk_rows[c]), :],
            recv[c].at[pl.ds(me * capacity, capacity)],
            a2a_recv.at[c],
        ).start()
        send_block(c, d, e, m + 1 - 2 * core)

    def steps(c, first, stop, gather=None, since=0):
        def step(r, carry):
            side = r // half
            rest = lax.rem(r, half)
            d2 = lax.rem(d + rest // x_count, n_dp)
            m2 = lax.rem(x + rest, x_count) * 2 + side
            for k in z_order:
                send_block(c, d2, es[k], m2)

            @pl.when(rest != 0)
            def _():
                send_block(c, d2, e, m2)

            gather_pieces(gather, r - first + since, PER_STEP)
            return carry

        lax.fori_loop(first, stop, step, 0)

    def gather_pieces(c, step, per_step):
        if c is None:
            return
        for k in range(per_step):
            t = step * per_step + k

            @pl.when(t < n_pieces)
            def _():
                gather_piece(c, t)

    def gather_piece(c, t):
        d2 = lax.rem(d + 1 + t % peers, n_dp)
        a = (t // peers) // splits
        part = pl.ds(((t // peers) % splits) * span, span)
        pltpu.make_async_remote_copy(
            src_ref=stage[c].at[a, part],
            dst_ref=out_hbm.at[a, part, pl.ds(d * quarter + first_row[c], chunk_rows[c]), :],
            send_sem=gather_send,
            recv_sem=gather_recv,
            device_id=(d2, e, m),
            device_id_type=MESH,
        ).start()

    def gather_own(c):
        pltpu.make_async_copy(
            stage[c], out_hbm.at[:, :, pl.ds(d * quarter + first_row[c], chunk_rows[c]), :], gather_recv
        ).start()

    for c in range(chunks):
        own_pair(c)
    for k in range(1, n_ex):
        pltpu.make_async_remote_copy(
            src_ref=enc,
            dst_ref=column_keys.at[e],
            send_sem=ids_send.at[0],
            recv_sem=ids_recv.at[0],
            device_id=(d, es[k], m),
            device_id_type=MESH,
        ).start()
    column_keys[pl.ds(e, 1)] = enc[...].reshape(1, 1, LANES)
    pl.semaphore_wait(column_sem, len(plane))
    steps(0, 0, half)
    others = column_keys.at[pl.ds(0, n_ex - 1)]
    pltpu.make_async_copy(others, others, ids_recv.at[0]).wait()
    here = pl.ds((d * n_mp + m) * n_ex, n_ex)
    for device in plane:
        pltpu.make_async_remote_copy(
            src_ref=column_keys,
            dst_ref=keys.at[here],
            send_sem=ids_send.at[1],
            recv_sem=ids_recv.at[1],
            device_id=device,
            device_id_type=MESH,
        ).start()
    keys[here] = column_keys[...]
    steps(0, half, early + rest_steps * core)
    if chunks > 1:
        steps(1, 0, AHEAD * core)
    base_copy.wait()

    far_keys = keys.at[pl.ds(0, n_dev - n_ex)]
    pltpu.make_async_copy(far_keys, far_keys, ids_recv.at[1]).wait()
    all_keys = keys[...].reshape(n_dev, LANES)
    q_mine = e * n_mp + m
    for g in range(n_dev // LANES):
        keys_t[:, g * LANES : (g + 1) * LANES] = all_keys[g * LANES : (g + 1) * LANES, :].T
    lane = lax.broadcasted_iota(jnp.int32, (1, LANES), 1)
    row_keys, row_slots = [], []
    for k in range(capacity):
        row = keys_t[pl.ds(q_mine * capacity + k, 1), :]
        for g in range(n_dev // LANES):
            row_keys.append(row[:, g * LANES : (g + 1) * LANES])
            row_slots.append((g * LANES + lane) * capacity + k)
    groups = len(row_keys)

    def down(row):
        return jnp.broadcast_to(row, (LANES, LANES)).T

    row_mixed = [a * n_slots + b for a, b in zip(row_keys, row_slots)]
    col_keys = [down(a) for a in row_keys]
    col_slots = [down(a) for a in row_slots]
    col_mixed = [a * n_slots + b for a, b in zip(col_keys, col_slots)]

    def count(masks):
        total = sum(jnp.where(x, 1, 0) for x in masks)
        return jnp.sum(total, axis=0, keepdims=True)

    ranks = [count([col_mixed[h] < row_mixed[g] for h in range(groups)]) for g in range(groups)]
    col_ranks = [down(a) for a in ranks]
    for g in range(groups):
        want = g * LANES + lane

        def at(values, rank):
            return jnp.sum(
                sum(jnp.where(r == rank, v, 0) for r, v in zip(col_ranks, values)), axis=0, keepdims=True
            )

        table[g : g + 1, :] = at(col_slots, want)
        same = jnp.logical_and(at(col_keys, want) == at(col_keys, want - 1), lane > 0)
        flags[g : g + 1, :] = jnp.where(same, 1.0, 0.0)
    begin = count([x < lane for x in col_keys])
    end = count([x <= lane for x in col_keys])
    table[groups : groups + 1, :] = jnp.maximum(end - 1, 0)
    flags[groups : groups + 1, :] = jnp.where(end > begin, 1.0, 0.0)
    for g in range(1, groups):
        cut = jnp.logical_and(begin < g * LANES, end > g * LANES)
        flags[groups + g : groups + g + 1, :] = jnp.where(cut, 1.0, 0.0)

    to_smem = [
        pltpu.make_async_copy(table, order, local_sem.at[1]),
        pltpu.make_async_copy(flags, weight, local_sem.at[5]),
    ]
    for copy in to_smem:
        copy.start()
    for copy in to_smem:
        copy.wait()

    def merge(c):
        rows, top = chunk_rows[c], first_row[c]
        pltpu.make_async_copy(recv[c], recv[c], a2a_recv.at[c]).wait()

        def add(l, running):
            result = []
            for g in range(groups):
                block = recv[c][order[g, l]].astype(jnp.float32)
                total = running[g] * weight[g, l] + block
                partial[g * LANES + l, 0:rows] = total
                result.append(total)
            return tuple(result)

        lax.fori_loop(0, LANES, add, (jnp.zeros((rows, LANES), jnp.float32),) * groups, unroll=UNROLL)
        edges = [partial[g * LANES - 1, 0:rows] for g in range(1, groups)]

        def finish(i, carry):
            a = i // row_blocks
            b = i % row_blocks
            for k in range(col_blocks):
                p = i * col_blocks + k
                total = partial[order[groups, p], 0:rows] * weight[groups, p]
                for g in range(1, groups):
                    total = total + edges[g - 1] * weight[groups + g, p]
                old = base_vmem[a, b, top : top + rows, k * LANES : (k + 1) * LANES]
                stage[c][a, b, :, k * LANES : (k + 1) * LANES] = (old.astype(jnp.float32) + total).astype(jnp.bfloat16)
            return carry

        lax.fori_loop(0, exp_dev * row_blocks, finish, 0, unroll=4)

    for c in range(chunks):
        merge(c)
        gather_own(c)
        steps(c, early + rest_steps * core, n_steps, gather=c)
        done = rest_steps * (1 - core)
        if c + 1 < chunks:
            steps(c + 1, AHEAD * core, early + rest_steps * core, gather=c, since=done)
            done = done + early + (rest_steps - AHEAD) * core
        if c + 2 < chunks:
            steps(c + 2, 0, AHEAD * core, gather=c, since=done)
            done = done + AHEAD * core

        def remaining(t, carry):
            gather_piece(c, t)
            return carry

        if c + 1 == chunks:
            lax.fori_loop(done * PER_STEP, n_pieces, remaining, 0)

    pltpu.make_async_copy(out_hbm, out_hbm, gather_recv).wait()
    sent = out_hbm.at[:, :, pl.ds(0, (n_dp - 1) * quarter), :]
    pltpu.make_async_copy(sent, sent, gather_send).wait()
    for c in range(chunks):
        sent = recv[c].at[pl.ds(0, n_slots - capacity)]
        pltpu.make_async_copy(sent, sent, a2a_send.at[c]).wait()
    pltpu.make_async_copy(others, others, ids_send.at[0]).wait()
    pltpu.make_async_copy(far_keys, far_keys, ids_send.at[1]).wait()


def body(base_weights, delta_blocks, block_ids, block_counts, owner_map):
    n_dp, n_ex, n_mp = (lax.axis_size(a) for a in ("dp", "expert", "mp"))
    n_dev = n_dp * n_ex * n_mp
    exp_dev, row_count, col_count = base_weights.shape
    block_size = delta_blocks.shape[1]
    row_blocks = row_count // block_size
    col_blocks = col_count // block_size
    capacity = delta_blocks.shape[0] // block_counts.shape[0]
    quarter = block_size // n_dp
    chunk_rows = CHUNKS
    n_slots = n_dev * capacity
    cfg = (n_dp, n_ex, n_mp, exp_dev, row_blocks, col_blocks, capacity, chunk_rows)
    shape = (exp_dev, row_blocks, block_size, col_count)
    filler = jnp.zeros((LANES - block_counts.shape[0] - owner_map.shape[0],), jnp.int32)
    lists = jnp.concatenate([block_ids, block_counts, owner_map, filler]).reshape(2, LANES)
    merged = pl.pallas_call(
        functools.partial(kernel, cfg),
        out_shape=jax.ShapeDtypeStruct(shape, jnp.bfloat16),
        in_specs=[
            pl.BlockSpec(memory_space=pltpu.VMEM),
            pl.BlockSpec(memory_space=pl.ANY),
            pl.BlockSpec(memory_space=pl.ANY),
        ],
        out_specs=pl.BlockSpec(memory_space=pl.ANY),
        scratch_shapes=[
            *[pltpu.VMEM((n_slots, rows, LANES), jnp.bfloat16) for rows in chunk_rows],
            *[pltpu.VMEM((exp_dev, row_blocks, rows, col_count), jnp.bfloat16) for rows in chunk_rows],
            pltpu.VMEM((exp_dev, row_blocks, quarter, col_count), jnp.bfloat16),
            pltpu.VMEM((n_slots, max(chunk_rows), LANES), jnp.float32),
            pltpu.VMEM((1, LANES), jnp.int32),
            pltpu.VMEM((n_ex, 1, LANES), jnp.int32),
            pltpu.VMEM((n_dev, 1, LANES), jnp.int32),
            pltpu.VMEM((LANES, n_dev), jnp.int32),
            pltpu.VMEM((8, LANES), jnp.int32),
            pltpu.VMEM((8, LANES), jnp.float32),
            pltpu.SMEM((8, LANES), jnp.int32),
            pltpu.SMEM((8, LANES), jnp.float32),
            pltpu.SemaphoreType.DMA((len(chunk_rows),)),
            pltpu.SemaphoreType.DMA((len(chunk_rows),)),
            pltpu.SemaphoreType.DMA((2,)),
            pltpu.SemaphoreType.DMA((2,)),
            pltpu.SemaphoreType.DMA((6,)),
            pltpu.SemaphoreType.DMA,
            pltpu.SemaphoreType.DMA,
            pltpu.SemaphoreType.REGULAR,
        ],
        compiler_params=pltpu.CompilerParams(
            collective_id=0, has_side_effects=True, vmem_limit_bytes=48 * 2**20
        ),
        name="merge_blocks",
    )(
        lists,
        base_weights.reshape(shape),
        delta_blocks,
    )
    return merged.reshape(base_weights.shape)


def solution(mesh):
    in_specs = (
        P("expert", None, "mp"),
        P(("dp", "expert", "mp"), None, None),
        P(("dp", "expert", "mp")),
        P(("dp", "expert", "mp")),
        P(),
    )
    out_specs = P("expert", None, "mp")
    return jax.shard_map(body, mesh=mesh, in_specs=in_specs, out_specs=out_specs, check_vma=False)
```

time: 135 us -> 122 us (0.904)
  the two profiles are of different devices: /device:TPU:32 before, /device:TPU:1 now
where the time goes in v2:
time: 122 us
  Pallas kernels  120 us (98%)
  local copies, waits for them, and re-layouts  1.93 us (2%)
    pallas_call x1, Pallas kernels, body(): pl.pallas_call(functools.partial(kernel, cfg), out_shape=jax.ShapeDtypeSt...  120 us

profile of v2, /device:TPU:1, one launch (start us, length us, event | category | flops | bytes accessed | tf_op | source)
XLA Modules:
  0.0 122.3 jit_solution(4488850117354807008)
XLA Ops:
  0.0 0.8 add_bitcast_fusion.lists
  0.8 119.6 %merge_blocks.1 = bf16[2,20,128,384]{3,2,1,0:T(8,128)(2,1)S(1)} custom-call(s32[2,128]{1,0:T(2,128)S(1)} %add_bitcast_fusion.lists, bf16[2,20,128,384]{3,2,1,0:T(8,128)(2,1)} %bitcast.5, bf16[128,128,128]{2,1,0:T(8,128)(2,1)} %delta_hbm.1), custom_call_target="tpu_custom_call" | custom-call | tf_op jit(solution)/shard_map/merge_blocks/pallas_call | solution.py:352
  120.4 1.9 %copy.7 = bf16[2,2560,384]{2,1,0:T(8,128)(2,1)} copy(bf16[2,2560,384]{2,1,0:T(8,128)(2,1)S(1)} %bitcast.4) | data formatting | bytes 7864320
  (1 shorter events, 0.0 us)

commit v3 on v2

--- a/solution.py
+++ b/solution.py
@@ -9,10 +9,12 @@
 
 MESH = pl.DeviceIdType.MESH
 CHUNKS = (8, 8, 8, 8)
-AHEAD = 12
+AHEAD = 14
 GATHER_SPLITS = 10
 PER_STEP = 4
-UNROLL = 4
+LAST_STEP = 30
+FIN_UNROLL = 8
+UNROLL = 8
 LANES = 128
 
 
@@ -121,10 +123,12 @@
     x_count = n_mp // 2
     x = m // 2
     core = m % 2
+    late = 1 - core
 
     n_steps = n_dp * n_mp
     last = chunks - 1
     peers = n_dp - 1
+    shifts = [n_dp // 2] + [i for i in range(1, n_dp) if i != n_dp // 2]
     splits = GATHER_SPLITS
     span = row_blocks // splits
     n_pieces = peers * exp_dev * splits
@@ -132,28 +136,33 @@
     early = half + AHEAD
     rest_steps = n_steps - early
 
-    def own_pair(c):
+    def known(c):
         pltpu.make_async_copy(
             delta_hbm.at[pl.ds(mine * capacity, capacity), pl.ds(d * quarter + first_row[c], chunk_rows[c]), :],
             recv[c].at[pl.ds(me * capacity, capacity)],
             a2a_recv.at[c],
         ).start()
+        for k in z_order:
+            send_block(c, d, es[k], m)
         send_block(c, d, e, m + 1 - 2 * core)
 
     def steps(c, first, stop, gather=None, since=0):
         def step(r, carry):
-            side = r // half
+            side = 1 - r // half
             rest = lax.rem(r, half)
             d2 = lax.rem(d + rest // x_count, n_dp)
             m2 = lax.rem(x + rest, x_count) * 2 + side
-            for k in z_order:
-                send_block(c, d2, es[k], m2)
+
+            @pl.when(r != half * late)
+            def _():
+                for k in z_order:
+                    send_block(c, d2, es[k], m2)
 
             @pl.when(rest != 0)
             def _():
                 send_block(c, d2, e, m2)
 
-            gather_pieces(gather, r - first + since, PER_STEP)
+            gather_pieces(gather, r - first + since, PER_STEP if gather != last else LAST_STEP)
             return carry
 
         lax.fori_loop(first, stop, step, 0)
@@ -181,13 +190,26 @@
             device_id_type=MESH,
         ).start()
 
+    def gather_row(c, i):
+        a = i // row_blocks
+        b = lax.rem(i, row_blocks)
+        for shift in shifts:
+            pltpu.make_async_remote_copy(
+                src_ref=stage[c].at[a, b],
+                dst_ref=out_hbm.at[a, b, pl.ds(d * quarter + first_row[c], chunk_rows[c]), :],
+                send_sem=gather_send,
+                recv_sem=gather_recv,
+                device_id=(ds[shift], e, m),
+                device_id_type=MESH,
+            ).start()
+
     def gather_own(c):
         pltpu.make_async_copy(
             stage[c], out_hbm.at[:, :, pl.ds(d * quarter + first_row[c], chunk_rows[c]), :], gather_recv
         ).start()
 
     for c in range(chunks):
-        own_pair(c)
+        known(c)
     for k in range(1, n_ex):
         pltpu.make_async_remote_copy(
             src_ref=enc,
@@ -213,9 +235,9 @@
             device_id_type=MESH,
         ).start()
     keys[here] = column_keys[...]
-    steps(0, half, early + rest_steps * core)
+    steps(0, half, early + rest_steps * late)
     if chunks > 1:
-        steps(1, 0, AHEAD * core)
+        steps(1, 0, AHEAD * late)
     base_copy.wait()
 
     far_keys = keys.at[pl.ds(0, n_dev - n_ex)]
@@ -301,28 +323,40 @@
                     total = total + edges[g - 1] * weight[groups + g, p]
                 old = base_vmem[a, b, top : top + rows, k * LANES : (k + 1) * LANES]
                 stage[c][a, b, :, k * LANES : (k + 1) * LANES] = (old.astype(jnp.float32) + total).astype(jnp.bfloat16)
+            if c == last:
+
+                @pl.when(jnp.logical_and(late == 1, i > 0))
+                def _():
+                    gather_row(c, i - 1)
+
             return carry
 
-        lax.fori_loop(0, exp_dev * row_blocks, finish, 0, unroll=4)
+        lax.fori_loop(0, exp_dev * row_blocks, finish, 0, unroll=FIN_UNROLL)
+        if c == last:
+
+            @pl.when(late == 1)
+            def _():
+                gather_row(c, exp_dev * row_blocks - 1)
+
 
     for c in range(chunks):
         merge(c)
         gather_own(c)
-        steps(c, early + rest_steps * core, n_steps, gather=c)
-        done = rest_steps * (1 - core)
-        if c + 1 < chunks:
-            steps(c + 1, AHEAD * core, early + rest_steps * core, gather=c, since=done)
-            done = done + early + (rest_steps - AHEAD) * core
+        if c == last:
+            steps(c, early + rest_steps * late, n_steps, gather=c)
+
+            def remaining(t, carry):
+                gather_piece(c, t)
+                return carry
+
+            lax.fori_loop(rest_steps * LAST_STEP + (n_pieces - rest_steps * LAST_STEP) * late, n_pieces, remaining, 0)
+            continue
+        steps(c, early + rest_steps * late, n_steps, gather=c)
+        done = rest_steps * core
+        steps(c + 1, AHEAD * late, early + rest_steps * late, gather=c, since=done)
         if c + 2 < chunks:
-            steps(c + 2, 0, AHEAD * core, gather=c, since=done)
-            done = done + AHEAD * core
-
-        def remaining(t, carry):
-            gather_piece(c, t)
-            return carry
-
-        if c + 1 == chunks:
-            lax.fori_loop(done * PER_STEP, n_pieces, remaining, 0)
+            done = done + early + (rest_steps - AHEAD) * late
+            steps(c + 2, 0, AHEAD * late, gather=c, since=done)
 
     pltpu.make_async_copy(out_hbm, out_hbm, gather_recv).wait()
     sent = out_hbm.at[:, :, pl.ds(0, (n_dp - 1) * quarter), :]

time: 122 us -> 117 us (0.959)
  the two profiles are of different devices: /device:TPU:1 before, /device:TPU:32 now
where the time goes in v3:
time: 117 us
  Pallas kernels  115 us (98%)
  local copies, waits for them, and re-layouts  1.93 us (2%)
    pallas_call x1, Pallas kernels, body(): pl.pallas_call(functools.partial(kernel, cfg), out_shape=jax.ShapeDtypeSt...  115 us

profile of v3, /device:TPU:32, one launch (start us, length us, event | category | flops | bytes accessed | tf_op | source)
XLA Modules:
  0.0 117.3 jit_solution(2615891444771548055)
XLA Ops:
  0.0 0.8 add_bitcast_fusion.lists
  0.8 114.6 %merge_blocks.1 = bf16[2,20,128,384]{3,2,1,0:T(8,128)(2,1)S(1)} custom-call(s32[2,128]{1,0:T(2,128)S(1)} %add_bitcast_fusion.lists, bf16[2,20,128,384]{3,2,1,0:T(8,128)(2,1)} %bitcast.5, bf16[128,128,128]{2,1,0:T(8,128)(2,1)} %delta_hbm.1), custom_call_target="tpu_custom_call" | custom-call | tf_op jit(solution)/shard_map/merge_blocks/pallas_call | solution.py:386
  115.4 1.9 %copy.7 = bf16[2,2560,384]{2,1,0:T(8,128)(2,1)} copy(bf16[2,2560,384]{2,1,0:T(8,128)(2,1)S(1)} %bitcast.4) | data formatting | bytes 7864320
  (1 shorter events, 0.0 us)

commit v4 on v3

--- a/solution.py
+++ b/solution.py
@@ -9,11 +9,15 @@
 
 MESH = pl.DeviceIdType.MESH
 CHUNKS = (8, 8, 8, 8)
-AHEAD = 14
+AHEAD = 16
 GATHER_SPLITS = 10
 PER_STEP = 4
-LAST_STEP = 30
+LAST_STEP = 10
 FIN_UNROLL = 8
+SEGMENTS = 4
+SEGMENT_PARTS = 2
+SEG_UNROLL = 10
+AHEAD_LAST = 10
 UNROLL = 8
 LANES = 128
 
@@ -49,6 +53,7 @@
         local_sem,
         gather_send,
         gather_recv,
+        near_recv,
         column_sem,
     ) = scratch[2 * chunks :]
     n_dev = n_dp * n_ex * n_mp
@@ -104,10 +109,9 @@
     for device in plane:
         pl.semaphore_signal(column_sem, inc=1, device_id=device, device_id_type=MESH)
 
-    z_order = []
-    for i in range(1, n_ex // 2):
+    z_order = [n_ex // 2]
+    for i in range(n_ex // 2 - 1, 0, -1):
         z_order += [i, n_ex - i]
-    z_order.append(n_ex // 2)
 
     def send_block(c, d2, e2, m2):
         q = e2 * n_mp + m2
@@ -128,7 +132,6 @@
     n_steps = n_dp * n_mp
     last = chunks - 1
     peers = n_dp - 1
-    shifts = [n_dp // 2] + [i for i in range(1, n_dp) if i != n_dp // 2]
     splits = GATHER_SPLITS
     span = row_blocks // splits
     n_pieces = peers * exp_dev * splits
@@ -158,9 +161,12 @@
                 for k in z_order:
                     send_block(c, d2, es[k], m2)
 
-            @pl.when(rest != 0)
-            def _():
-                send_block(c, d2, e, m2)
+            if c == 0:
+
+                @pl.when(rest != 0)
+                def _():
+                    for other in range(chunks):
+                        send_block(other, d2, e, m2)
 
             gather_pieces(gather, r - first + since, PER_STEP if gather != last else LAST_STEP)
             return carry
@@ -173,35 +179,52 @@
         for k in range(per_step):
             t = step * per_step + k
 
-            @pl.when(t < n_pieces)
+            @pl.when(t < pieces_of[c])
             def _():
                 gather_piece(c, t)
 
+    def rows_of(device, c):
+        return pl.ds(device * quarter + first_row[c], chunk_rows[c])
+
+    left, right = ds[n_dp - 1], ds[1]
+    pieces_of = [exp_dev * splits * (peers if c == last else 2) for c in range(chunks)]
+
     def gather_piece(c, t):
-        d2 = lax.rem(d + 1 + t % peers, n_dp)
-        a = (t // peers) // splits
-        part = pl.ds(((t // peers) % splits) * span, span)
+        fan = peers if c == last else 2
+        piece = t // fan
+        a = piece // splits
+        part = pl.ds((piece % splits) * span, span)
+        to = lax.rem(d + 1 + t % fan * (1 if c == last else n_dp - 2), n_dp)
+        arrival = gather_recv if c == last else near_recv.at[c * 2 + t % fan]
         pltpu.make_async_remote_copy(
             src_ref=stage[c].at[a, part],
-            dst_ref=out_hbm.at[a, part, pl.ds(d * quarter + first_row[c], chunk_rows[c]), :],
+            dst_ref=out_hbm.at[a, part, rows_of(d, c), :],
             send_sem=gather_send,
-            recv_sem=gather_recv,
-            device_id=(d2, e, m),
+            recv_sem=arrival,
+            device_id=(to, e, m),
             device_id_type=MESH,
         ).start()
 
-    def gather_row(c, i):
-        a = i // row_blocks
-        b = lax.rem(i, row_blocks)
-        for shift in shifts:
-            pltpu.make_async_remote_copy(
-                src_ref=stage[c].at[a, b],
-                dst_ref=out_hbm.at[a, b, pl.ds(d * quarter + first_row[c], chunk_rows[c]), :],
-                send_sem=gather_send,
-                recv_sem=gather_recv,
-                device_id=(ds[shift], e, m),
-                device_id_type=MESH,
-            ).start()
+    def forward(c):
+        for side in range(2):
+            pltpu.make_async_copy(stage[c], stage[c], near_recv.at[c * 2 + side]).wait()
+
+        def step(t, carry):
+            part = pl.ds(t * span, span)
+            for a in range(exp_dev):
+                source, to = (left, right) if a < exp_dev // 2 else (right, left)
+                block = out_hbm.at[a, part, rows_of(source, c), :]
+                pltpu.make_async_remote_copy(
+                    src_ref=block,
+                    dst_ref=block,
+                    send_sem=gather_send,
+                    recv_sem=gather_recv,
+                    device_id=(to, e, m),
+                    device_id_type=MESH,
+                ).start()
+            return carry
+
+        lax.fori_loop(0, splits, step, 0)
 
     def gather_own(c):
         pltpu.make_async_copy(
@@ -323,42 +346,62 @@
                     total = total + edges[g - 1] * weight[groups + g, p]
                 old = base_vmem[a, b, top : top + rows, k * LANES : (k + 1) * LANES]
                 stage[c][a, b, :, k * LANES : (k + 1) * LANES] = (old.astype(jnp.float32) + total).astype(jnp.bfloat16)
-            if c == last:
-
-                @pl.when(jnp.logical_and(late == 1, i > 0))
-                def _():
-                    gather_row(c, i - 1)
-
             return carry
 
-        lax.fori_loop(0, exp_dev * row_blocks, finish, 0, unroll=FIN_UNROLL)
-        if c == last:
-
+        if c < last:
+            lax.fori_loop(0, exp_dev * row_blocks, finish, 0, unroll=FIN_UNROLL)
+            return
+
+        def send_segment(i):
             @pl.when(late == 1)
             def _():
-                gather_row(c, exp_dev * row_blocks - 1)
-
+                for part in range(SEGMENT_PARTS):
+                    first = (i * SEGMENT_PARTS + part) * (exp_dev * row_blocks // SEGMENTS // SEGMENT_PARTS)
+                    a, b = divmod(first, row_blocks)
+                    blocks = pl.ds(b, exp_dev * row_blocks // SEGMENTS // SEGMENT_PARTS)
+                    for shift in [n_dp // 2] + [k for k in range(1, n_dp) if k != n_dp // 2]:
+                        pltpu.make_async_remote_copy(
+                            src_ref=stage[c].at[a, blocks],
+                            dst_ref=out_hbm.at[a, blocks, rows_of(d, c), :],
+                            send_sem=gather_send,
+                            recv_sem=gather_recv,
+                            device_id=(ds[shift], e, m),
+                            device_id_type=MESH,
+                        ).start()
+
+        size = exp_dev * row_blocks // SEGMENTS
+        for i in range(SEGMENTS):
+            lax.fori_loop(i * size, (i + 1) * size, finish, 0, unroll=SEG_UNROLL)
+            if i > 0:
+                send_segment(i - 1)
+        send_segment(SEGMENTS - 1)
 
     for c in range(chunks):
+        if c > 0:
+            forward(c - 1)
         merge(c)
         gather_own(c)
         if c == last:
-            steps(c, early + rest_steps * late, n_steps, gather=c)
+            stop = half + AHEAD_LAST
+            rest_last = n_steps - stop
+            steps(c, stop + rest_last * late, n_steps, gather=c)
 
             def remaining(t, carry):
                 gather_piece(c, t)
                 return carry
 
-            lax.fori_loop(rest_steps * LAST_STEP + (n_pieces - rest_steps * LAST_STEP) * late, n_pieces, remaining, 0)
+            lax.fori_loop(rest_last * LAST_STEP + (n_pieces - rest_last * LAST_STEP) * late, n_pieces, remaining, 0)
             continue
         steps(c, early + rest_steps * late, n_steps, gather=c)
         done = rest_steps * core
-        steps(c + 1, AHEAD * late, early + rest_steps * late, gather=c, since=done)
+        stop = early if c + 1 < last else half + AHEAD_LAST
+        steps(c + 1, AHEAD * late, stop + (n_steps - stop) * late, gather=c, since=done)
         if c + 2 < chunks:
             done = done + early + (rest_steps - AHEAD) * late
             steps(c + 2, 0, AHEAD * late, gather=c, since=done)
 
-    pltpu.make_async_copy(out_hbm, out_hbm, gather_recv).wait()
+    waited = out_hbm.at[:, :, pl.ds(0, n_dp * quarter - 2 * sum(chunk_rows[:last])), :]
+    pltpu.make_async_copy(waited, waited, gather_recv).wait()
     sent = out_hbm.at[:, :, pl.ds(0, (n_dp - 1) * quarter), :]
     pltpu.make_async_copy(sent, sent, gather_send).wait()
     for c in range(chunks):
@@ -412,6 +455,7 @@
             pltpu.SemaphoreType.DMA((6,)),
             pltpu.SemaphoreType.DMA,
             pltpu.SemaphoreType.DMA,
+            pltpu.SemaphoreType.DMA((2 * len(chunk_rows) - 2,)),
             pltpu.SemaphoreType.REGULAR,
         ],
         compiler_params=pltpu.CompilerParams(

time: 117 us -> 117 us (level)
  no operation moved by 1% of the time
where the time goes in v4:
time: 117 us
  Pallas kernels  114 us (97%)
  local copies, waits for them, and re-layouts  1.93 us (2%)
    pallas_call x1, Pallas kernels, body(): pl.pallas_call(functools.partial(kernel, cfg), out_shape=jax.ShapeDtypeSt...  114 us

profile of v4, /device:TPU:32, one launch (start us, length us, event | category | flops | bytes accessed | tf_op | source)
XLA Modules:
  0.0 117.0 jit_solution(17227979664959898697)
XLA Ops:
  0.0 0.8 add_bitcast_fusion.lists
  0.8 114.3 %merge_blocks.1 = bf16[2,20,128,384]{3,2,1,0:T(8,128)(2,1)S(1)} custom-call(s32[2,128]{1,0:T(2,128)S(1)} %add_bitcast_fusion.lists, bf16[2,20,128,384]{3,2,1,0:T(8,128)(2,1)} %bitcast.5, bf16[128,128,128]{2,1,0:T(8,128)(2,1)} %delta_hbm.1), custom_call_target="tpu_custom_call" | custom-call | tf_op jit(solution)/shard_map/merge_blocks/pallas_call | solution.py:429
  115.1 1.9 %copy.7 = bf16[2,2560,384]{2,1,0:T(8,128)(2,1)} copy(bf16[2,2560,384]{2,1,0:T(8,128)(2,1)S(1)} %bitcast.4) | data formatting | bytes 7864320
  (1 shorter events, 0.0 us)

commit v5 on v4

--- a/solution.py
+++ b/solution.py
@@ -18,7 +18,7 @@
 SEGMENT_PARTS = 2
 SEG_UNROLL = 10
 AHEAD_LAST = 10
-UNROLL = 8
+UNROLL = 16
 LANES = 128
 
 

time: 117 us -> 117 us (level)
  no operation moved by 1% of the time
where the time goes in v5:
time: 117 us
  Pallas kernels  114 us (97%)
  local copies, waits for them, and re-layouts  1.93 us (2%)
    pallas_call x1, Pallas kernels, body(): pl.pallas_call(functools.partial(kernel, cfg), out_shape=jax.ShapeDtypeSt...  114 us

profile of v5, /device:TPU:32, one launch (start us, length us, event | category | flops | bytes accessed | tf_op | source)
XLA Modules:
  0.0 117.1 jit_solution(5455664477219142201)
XLA Ops:
  0.0 0.8 add_bitcast_fusion.lists
  0.8 114.4 %merge_blocks.1 = bf16[2,20,128,384]{3,2,1,0:T(8,128)(2,1)S(1)} custom-call(s32[2,128]{1,0:T(2,128)S(1)} %add_bitcast_fusion.lists, bf16[2,20,128,384]{3,2,1,0:T(8,128)(2,1)} %bitcast.5, bf16[128,128,128]{2,1,0:T(8,128)(2,1)} %delta_hbm.1), custom_call_target="tpu_custom_call" | custom-call | tf_op jit(solution)/shard_map/merge_blocks/pallas_call | solution.py:429
  115.1 1.9 %copy.7 = bf16[2,2560,384]{2,1,0:T(8,128)(2,1)} copy(bf16[2,2560,384]{2,1,0:T(8,128)(2,1)S(1)} %bitcast.4) | data formatting | bytes 7864320
  (1 shorter events, 0.0 us)
